TPU v7x, 256 devices: a whole 4x4x8 slice. The times are simulated.
256 devices in a mesh: slab: 64 (over y, z, core), tile: 4 (over x).
Axes of the slice: x: 4, y: 4, z: 8, core: 2. Of those that a mesh axis runs over, the one named last changes fastest.
Arguments:
- grid: bfloat16 [512, 256, 1024], P('slab', 'tile'), may hold values from -6 to 6
- type_table: float32 [16, 8], replicated, may hold values from -4 to 4
- counts: int32 [4096], P(('slab', 'tile')), may hold values from 10 to 120
- types: int32 [4096, 128], P(('slab', 'tile')), may hold values from 0 to 15
- offsets: float32 [4096, 3, 128], P(('slab', 'tile')), may hold values from 0 to 0.999
- route: int32 [4096, 1], P('slab'), may hold values from 0 to 63; in each aligned block of 64 rows (0 to 63, 64 to 127, ...) at most 2 rows name the same one
- base_y: int32 [4096], P(('slab', 'tile')), may hold values from 0 to 223
- base_z: int32 [4096], P(('slab', 'tile')), may hold values from 0 to 95
Outputs:
- energy: float32 [4096], P(('slab', 'tile'))
Inputs may be any that keep to these rules, and one draw needn't show every extreme that they name: `route`: among the rows of one aligned block of 64 poses (those starting on one group of tile devices), at most 2 name the same slab.
All inputs are finite; a program needn't handle non-finite values.
Results may differ from a plain program's by a relative error of at most 0.0003.
Values may be sent and summed in bfloat16 or wider, within the bound.
No kernel may reach another device: no remote copies, remote signals or barrier semaphores. Data moves between devices by JAX's collectives and lax.ppermute only.
A program may use at most 64 MiB of HBM per device.

v0:
```python
import jax
import jax.numpy as jnp
from jax import lax
from jax.sharding import PartitionSpec as P

SPAN = 32


def from_behind(shard, axis, by):
    devices = lax.axis_size(axis)
    pairs = [(i, i + by) for i in range(devices) if 0 <= i + by < devices]
    return lax.ppermute(shard, axis, pairs)


def sent_to_all(shard, axis):
    copies = jnp.broadcast_to(shard, (lax.axis_size(axis), *shard.shape))
    return lax.all_to_all(copies, axis, split_axis=0, concat_axis=0, tiled=True)


def in_order(tiles, dim):
    tiles = jnp.moveaxis(tiles, 0, dim)
    dims = tiles.shape
    return tiles.reshape(*dims[:dim], dims[dim] * dims[dim + 1], *dims[dim + 2 :])


def collect(shard, axis, dim):
    tiles = sent_to_all(shard, axis)
    return in_order(tiles, dim)


def split_up(shard, dim, devices):
    dims = shard.shape
    tiles = shard.reshape(*dims[:dim], devices, dims[dim] // devices, *dims[dim + 1 :])
    return jnp.moveaxis(tiles, dim, 0)


def sum_at_owner(shard, axis, dim):
    devices = lax.axis_size(axis)
    tiles = lax.all_to_all(split_up(shard, dim, devices), axis, 0, 0, tiled=True)
    return jnp.sum(tiles, axis=0)


def build_payload(type_table, counts, types, offsets, base_y, base_z, cells_x):
    atom_slots = types.shape[1]
    onehot = (types[:, :, None] == jnp.arange(type_table.shape[0])[None, None, :]).astype(
        jnp.float32
    )
    typed = jnp.einsum("pat,tc->pca", onehot, type_table, precision=lax.Precision.HIGHEST)
    live = (jnp.arange(atom_slots)[None, :] < counts[:, None]).astype(jnp.float32) / counts[
        :, None
    ].astype(jnp.float32)
    coef = typed * live[:, None, :]
    local_x = offsets[:, 0, :] * (cells_x - 1)
    pos_y = base_y[:, None].astype(jnp.float32) + offsets[:, 1, :] * SPAN
    pos_z = base_z[:, None].astype(jnp.float32) + offsets[:, 2, :] * SPAN
    return jnp.concatenate(
        [local_x[:, None, :], pos_y[:, None, :], pos_z[:, None, :], coef], axis=1
    )


def slot_ranks(targets):
    count = targets.shape[0]
    order = jnp.arange(count)
    same = (targets[:, None] == targets[None, :]) & (order[:, None] > order[None, :])
    return jnp.sum(same.astype(jnp.int32), axis=1)


def slot_table(targets, ranks, slabs, slots):
    count = targets.shape[0]
    hits = (
        (targets[None, None, :] == jnp.arange(slabs)[:, None, None])
        & (ranks[None, None, :] == jnp.arange(slots)[None, :, None])
    ).astype(jnp.int32)
    owner = jnp.sum(hits * jnp.arange(count)[None, None, :], axis=2)
    filled = jnp.sum(hits, axis=2)
    return (owner.reshape(-1), filled.reshape(-1))


def corner_table(grid, rim, cells_x, cells_y, cells_z, chans):
    extended = jnp.concatenate([grid, rim], axis=1).reshape(cells_x, cells_y + 1, cells_z, chans)
    paired = jnp.concatenate([extended[:, :, :-1, :], extended[:, :, 1:, :]], axis=3)
    square = jnp.concatenate([paired[:, :-1], paired[:, 1:]], axis=3)
    return square.reshape(cells_x * cells_y * (cells_z - 1), 4 * chans)


def score(slots_data, table, tile_index, cells_x, cells_y, cells_z, chans):
    local_x = slots_data[:, 0, :]
    local_y = slots_data[:, 1, :] - (tile_index * cells_y).astype(jnp.float32)
    pos_z = slots_data[:, 2, :]
    coef = jnp.swapaxes(slots_data[:, 3:, :], 1, 2)
    floor_x = jnp.floor(local_x)
    floor_y = jnp.floor(local_y)
    floor_z = jnp.floor(pos_z)
    inside = ((floor_y >= 0) & (floor_y < cells_y)).astype(jnp.float32)
    cell_x = jnp.clip(floor_x, 0, cells_x - 2)
    cell_y = jnp.clip(floor_y, 0, cells_y - 1)
    cell_z = jnp.clip(floor_z, 0, cells_z - 2)
    frac_x = local_x - cell_x
    frac_y = local_y - cell_y
    frac_z = pos_z - cell_z
    int_x = cell_x.astype(jnp.int32)
    int_y = cell_y.astype(jnp.int32)
    int_z = cell_z.astype(jnp.int32)
    quarter = jnp.stack(
        [
            (1.0 - frac_y) * (1.0 - frac_z),
            (1.0 - frac_y) * frac_z,
            frac_y * (1.0 - frac_z),
            frac_y * frac_z,
        ],
        axis=2,
    )
    lines = cells_y * (cells_z - 1)
    index = int_x * lines + int_y * (cells_z - 1) + int_z
    total = jnp.zeros(local_x.shape + (chans,), jnp.float32)
    for step_x in range(2):
        factor = frac_x if step_x else 1.0 - frac_x
        values = jnp.take(table, index + step_x * lines, axis=0).astype(jnp.float32)
        values = values.reshape(local_x.shape + (4, chans))
        mixed = jnp.sum(quarter[:, :, :, None] * values, axis=2)
        total = total + factor[:, :, None] * mixed
    return jnp.sum(jnp.sum(total * coef, axis=2) * inside, axis=1)


def body(grid, type_table, counts, types, offsets, route, base_y, base_z):
    tile_index = lax.axis_index("tile")
    slabs = lax.axis_size("slab")
    pose_count = counts.shape[0]
    atom_slots = types.shape[1]
    chans = type_table.shape[1]
    cells_x, cells_y, wide_z = grid.shape
    cells_z = wide_z // chans
    capacity = max(2, 8 * pose_count // slabs)
    rim = from_behind(grid[:, :1, :], "tile", -1)
    table = corner_table(grid, rim, cells_x, cells_y, cells_z, chans)
    targets = route[:, 0]
    ranks = slot_ranks(targets)
    owner, filled = slot_table(targets, ranks, slabs, capacity)
    used = filled.astype(jnp.float32)
    payload = build_payload(type_table, counts, types, offsets, base_y, base_z, cells_x)
    rows = payload.shape[1]
    grouped = collect(payload, "tile", 0)
    outgoing = (jnp.take(grouped, owner, axis=0) * used[:, None, None]).reshape(
        slabs, capacity, rows, atom_slots
    )
    incoming = lax.all_to_all(outgoing, "slab", split_axis=0, concat_axis=0, tiled=True)
    slots_data = incoming.reshape(slabs * capacity, rows, atom_slots)
    partial_value = score(slots_data, table, tile_index, cells_x, cells_y, cells_z, chans)
    returned = lax.all_to_all(
        partial_value.reshape(slabs, capacity), "slab", split_axis=0, concat_axis=0, tiled=True
    )
    per_pose = jnp.take(returned.reshape(-1), targets * capacity + ranks, axis=0)
    return sum_at_owner(per_pose, "tile", 0)


def solution(mesh):
    in_specs = (
        P("slab", "tile", None),
        P(),
        P(("slab", "tile")),
        P(("slab", "tile"), None),
        P(("slab", "tile"), None, None),
        P("slab", None),
        P(("slab", "tile")),
        P(("slab", "tile")),
    )
    out_specs = P(("slab", "tile"))
    return jax.shard_map(body, mesh=mesh, in_specs=in_specs, out_specs=out_specs, check_vma=False)
```

profile of v0, /device:TPU:1, one launch (start us, length us, event | category | flops | bytes accessed | tf_op | source)
XLA Modules:
  0.0 247.1 jit_solution(3430725706523198417)
XLA Ops:
  0.0 0.7 convert_element_type.63
  0.7 0.7 convert_element_type.64
  1.3 0.7 convert_element_type.66
  2.0 0.7 convert_divide_fusion
  2.7 0.8 slice_multiply_fusion
  3.5 0.9 fusion.3
  4.5 0.8 broadcast_in_dim.20
  5.2 4.8 %all-to-all-start = ((f32[4,16,11,128]{3,1,2,0:T(8,128)}), f32[4,16,11,128]{3,1,2,0:T(8,128)}, u32[]{:S(2)}, u32[]{:S(2)}) async-start(f32[4,16,11,128]{3,1,2,0:T(8,128)} %broadcast_in_dim.20), calls=%async_computation | async-start | bytes 720896 | tf_op jit(solution)/shard_map/all_to_all | solution.py:17
  10.1 0.9 slice.42
  11.0 1.3 collective-permute-start
  12.3 0.9 convert_reduce_fusion
  13.2 0.7 iota_compare_fusion.2
  13.9 0.2 fusion.8
  14.0 0.1 copy.134
  14.2 0.7 and_reduce_fusion
  14.8 0.1 reshape.337
  15.0 0.1 copy.128
  15.2 0.9 collective-permute-done
  16.2 1.4 pad_maximum_fusion.1
  17.5 1.7 copy.139
  19.2 1.1 copy.133
  20.4 1.7 gather_fusion
  22.1 2.5 %fusion.4 = f32[64,2,11,128]{3,1,2,0:T(2,128)} fusion(f32[64,2,11,128]{3,2,1,0:T(8,128)} %bitcast.98, pred[64,2]{1,0:T(8,128)(4,1)S(1)} %copy.128, f32[64,2]{1,0:T(8,128)S(1)} %copy.136), kind=kLoop, calls=%fused_computation.15 | loop fusion | flops 360448 | bytes 1442432 | tf_op jit(solution)/shard_map/mul | solution.py:143
  24.6 13.5 %all-to-all-start.1 = ((f32[64,2,11,128]{3,1,2,0:T(2,128)}), f32[64,2,11,128]{3,1,2,0:T(2,128)S(1)}, u32[]{:S(2)}, u32[]{:S(2)}) async-start(f32[64,2,11,128]{3,1,2,0:T(2,128)} %fusion.4), calls=%async_computation.1 | async-start | bytes 1441792 | tf_op jit(solution)/shard_map/all_to_all | solution.py:146
  38.1 0.5 fusion.17
  38.7 1.0 slice_maximum_fusion
  39.7 6.2 %fusion = bf16[8,64,127,32]{1,3,2,0:T(8,128)(2,1)} fusion(bf16[8,65,127,8]{1,3,2,0:T(8,128)(2,1)S(1)} %get-tuple-element.15, bf16[8,65,127,8]{1,3,2,0:T(8,128)(2,1)S(1)} %get-tuple-element.14, bf16[8,64,127,16]{1,3,2,0:T(8,128)(2,1)S(1)} %slice_maximum_fusion), kind=kLoop, calls=%fused_computation.5 | loop fusion | flops 12484608 | bytes 8355584 | tf_op jit(solution)/shard_map/concatenate | solution.py:82
  45.9 10.0 %copy.140 = bf16[8,64,127,32]{2,1,0,3:T(8,128)(2,1)} copy(bf16[8,64,127,32]{1,3,2,0:T(8,128)(2,1)} %fusion) | data formatting | bytes 8323072 | tf_op jit(solution)/shard_map/concatenate | solution.py:82
  55.9 8.5 %reshape.340 = bf16[65024,32]{0,1:T(8,128)(2,1)} reshape(bf16[8,64,127,32]{2,1,0,3:T(8,128)(2,1)} %copy.140) | data formatting | bytes 8323072 | tf_op jit(solution)/shard_map/reshape | solution.py:83
  64.5 13.5 %copy.141 = bf16[65024,32]{1,0:T(8,128)(2,1)} copy(bf16[65024,32]{0,1:T(8,128)(2,1)} %reshape.340) | data formatting | bytes 8323072 | tf_op jit(solution)/shard_map/reshape | solution.py:83
  78.0 0.3 copy.137
  78.6 0.9 copy.138
  79.4 62.9 %gather_fusion.3 = bf16[16384,32]{1,0:T(8,128)(2,1)} fusion(bf16[65024,32]{1,0:T(8,128)(2,1)} %copy.141, s32[16384]{0:T(1024)S(1)} %get-tuple-element.22), kind=kCustom, calls=%fused_computation.1.clone | custom fusion | bytes 2162688 | tf_op jit(solution)/shard_map/jit(_take)/gather | solution.py:118
  142.4 3.6 %copy.144 = bf16[128,128,32]{1,2,0:T(8,128)(2,1)S(1)} copy(bf16[128,128,32]{2,1,0:T(8,128)(2,1)} %bitcast.96) | data formatting | bytes 2097152 | tf_op jit(solution)/shard_map/jit(_take)/gather | solution.py:118
  146.0 62.9 %gather_fusion.2 = bf16[16384,32]{1,0:T(8,128)(2,1)} fusion(bf16[65024,32]{1,0:T(8,128)(2,1)} %copy.141, s32[16384]{0:T(1024)S(1)} %get-tuple-element.23), kind=kCustom, calls=%fused_computation.clone | custom fusion | bytes 2162688 | tf_op jit(solution)/shard_map/jit(_take)/gather | solution.py:118
  208.9 3.8 %copy.142 = bf16[128,128,32]{1,2,0:T(8,128)(2,1)S(1)} copy(bf16[128,128,32]{2,1,0:T(8,128)(2,1)} %bitcast.95) | data formatting | bytes 2097152 | tf_op jit(solution)/shard_map/jit(_take)/gather | solution.py:118
  212.7 2.4 fusion.2
  215.1 0.6 fusion.6
  215.6 0.1 select_reduce_fusion
  215.7 0.8 all_to_all.18
  216.5 10.3 %all-to-all-start.2 = ((f32[64,1,2]{2,1,0:T(1,128)}), f32[64,1,2]{2,1,0:T(1,128)S(1)}, u32[]{:S(2)}, u32[]{:S(2)}) async-start(f32[64,1,2]{2,1,0:T(1,128)} %bitcast.25), calls=%async_computation.2 | async-start | bytes 65536 | tf_op jit(solution)/shard_map/all_to_all | solution.py:149
  226.9 9.2 %all-to-all-done.2 = f32[64,1,2]{2,1,0:T(1,128)S(1)} async-done(((f32[64,1,2]{2,1,0:T(1,128)}), f32[64,1,2]{2,1,0:T(1,128)S(1)}, u32[]{:S(2)}, u32[]{:S(2)}) %all-to-all-start.2) | async-done | bytes 544 | tf_op jit(solution)/shard_map/all_to_all | solution.py:149
  236.1 0.5 broadcast.318
  236.6 0.7 reduce.8
  237.4 0.1 reshape.345
  237.5 0.8 gather_fusion.1
  238.4 8.2 %all_to_all.25 = f32[4,1,16]{2,1,0:T(1,128)S(1)} all-to-all(f32[4,1,16]{2,1,0:T(1,128)S(1)} %bitcast.107), channel_id=1, replica_groups=mesh['slab'=64,'tile'=4] {'tile'}, dimensions={0} | all-to-all | bytes 512 | tf_op jit(solution)/shard_map/all_to_all | solution.py:39
  246.6 0.5 reduce_sum.82
  (23 shorter events, 0.6 us)
Async XLA Ops:
  0.0 3.5 %copy-start = (f32[16,8]{0,1:T(8,128)S(1)}, f32[16,8]{0,1:T(8,128)}, u32[]{:S(2)}) copy-start(f32[16,8]{0,1:T(8,128)} %param.11) | copy-start | bytes 1540
  5.2 14.0 %all-to-all-start = ((f32[4,16,11,128]{3,1,2,0:T(8,128)}), f32[4,16,11,128]{3,1,2,0:T(8,128)}, u32[]{:S(2)}, u32[]{:S(2)}) async-start(f32[4,16,11,128]{3,1,2,0:T(8,128)} %broadcast_in_dim.20), calls=%async_computation | async-start | bytes 720896 | tf_op jit(solution)/shard_map/all_to_all | solution.py:17
  11.0 5.2 %collective-permute-start = (bf16[8,1,1024]{2,1,0:T(2,128)(2,1)S(1)}, bf16[8,1,1024]{2,1,0:T(2,128)(2,1)S(1)}, u32[]{:S(2)}, u32[]{:S(2)}) collective-permute-start(bf16[8,1,1024]{2,1,0:T(2,128)(2,1)S(1)} %slice.42), channel_id=1, source_target_pairs={{1,0},{2,1},{3,2},{5,4},{6,5},{7,6},{9,8},{10,9},{11,10},{13,12},{... | collective-permute-start | bytes 49160 | tf_op jit(solution)/shard_map/ppermute | solution.py:12
  24.6 53.3 %all-to-all-start.1 = ((f32[64,2,11,128]{3,1,2,0:T(2,128)}), f32[64,2,11,128]{3,1,2,0:T(2,128)S(1)}, u32[]{:S(2)}, u32[]{:S(2)}) async-start(f32[64,2,11,128]{3,1,2,0:T(2,128)} %fusion.4), calls=%async_computation.1 | async-start | bytes 1441792 | tf_op jit(solution)/shard_map/all_to_all | solution.py:146
  216.5 19.6 %all-to-all-start.2 = ((f32[64,1,2]{2,1,0:T(1,128)}), f32[64,1,2]{2,1,0:T(1,128)S(1)}, u32[]{:S(2)}, u32[]{:S(2)}) async-start(f32[64,1,2]{2,1,0:T(1,128)} %bitcast.25), calls=%async_computation.2 | async-start | bytes 65536 | tf_op jit(solution)/shard_map/all_to_all | solution.py:149
where the time goes:
time: 249 us; the launch traced here: 247 us
  local copies, waits for them, and re-layouts  176 us (71%)
  starting transfers between devices  29.9 us (12%)
  other arithmetic  21.6 us (9%)
  waiting for transfers between devices  10.2 us (4%)
  blocking collectives  8.23 us (3%)
    gather x4, local copies, waits for them, and re-layouts, score(): values = jnp.take(table, index + step_x * lines, axis=0).astype(jnp.float32)  133 us
    reshape x2, local copies, waits for them, and re-layouts, corner_table(): return square.reshape(cells_x * cells_y * (cells_z - 1), 4 * chans)  22 us
    all_to_all x1, starting transfers between devices, body(): lax.all_to_all(outgoing, 'slab', split_axis=0, concat_axis=0, tiled=True)  13.5 us
    all_to_all x1, starting transfers between devices, body(): lax.all_to_all(partial_value.reshape(slabs, capacity), 'slab', split_axis...  10.3 us
    concatenate x1, local copies, waits for them, and re-layouts, corner_table(): square = jnp.concatenate([paired[:, :-1], paired[:, 1:]], axis=3)  10 us
    all_to_all x1, waiting for transfers between devices, body(): lax.all_to_all(partial_value.reshape(slabs, capacity), 'slab', split_axis...  9.21 us
    all_to_all x1, blocking collectives, sum_at_owner(): lax.all_to_all(split_up(shard, dim, devices), axis, 0, 0, tiled=True)  8.23 us
    concatenate x1, other arithmetic, corner_table(): square = jnp.concatenate([paired[:, :-1], paired[:, 1:]], axis=3)  6.22 us
  transfers between devices with their start and end apart: 4, of which 2 were waited for; matrix products, arithmetic and copies ran while one was open for 19% of the time, Pallas kernels for 0%

commit v1 on v0

v1 whole, which is shorter than its diff:
```python
import jax
import jax.numpy as jnp
from jax import lax
from jax.experimental import pallas as pl
from jax.experimental.pallas import tpu as pltpu
from jax.sharding import PartitionSpec as P

SPAN = 32
SLOTS = 2
YB = 16
ZB = 16
LIVE_LANES = 120
DEAD = 99.0
BIG = 1.0e6


def smem():
    return pl.BlockSpec(memory_space=pltpu.SMEM)


def vmem():
    return pl.BlockSpec(memory_space=pltpu.VMEM)


def hbm():
    return pl.BlockSpec(memory_space=pl.ANY)


def send_kernel(tile, route, counts, base_y, base_z, types, offsets, out, spot, used, *, span_x):
    poses, atoms = types.shape
    slabs = out.shape[0]
    out[...] = jnp.zeros(out.shape, jnp.float32)

    def clear(i, carry):
        used[i] = 0
        return carry

    lax.fori_loop(0, slabs, clear, 0)
    lane = lax.broadcasted_iota(jnp.int32, (1, atoms), 1)
    row = lax.broadcasted_iota(jnp.int32, (8, atoms), 0)
    first = tile[0] * poses
    for p in range(poses):
        slab = route[first + p, 0]
        slot = used[slab]
        used[slab] = slot + 1
        spot[p] = SLOTS * slab + slot
        off = offsets[p]
        x = off[0:1] * span_x
        y = base_y[p].astype(jnp.float32) + off[1:2] * SPAN
        z = base_z[p].astype(jnp.float32) + off[2:3] * SPAN
        kind = jnp.where(lane < counts[p], types[p : p + 1].astype(jnp.float32), DEAD)
        kind = jnp.where(lane == LIVE_LANES, 1.0, kind)
        kind = jnp.where(lane == LIVE_LANES + 1, (base_y[p] // YB).astype(jnp.float32), kind)
        kind = jnp.where(lane == LIVE_LANES + 2, (base_z[p] // ZB).astype(jnp.float32), kind)
        block = jnp.concatenate([x, y, z, kind, x, y, z, kind], axis=0)
        out[slab] = jnp.where(row // 4 == slot, block, out[slab])


def hat(distance):
    return jnp.maximum(1.0 - jnp.abs(distance), 0.0)


def score_pose(key, incoming, table, cells, sums):
    slabs = incoming.shape[0]
    number = key // 128
    code = key % 128
    block_y = code // 8
    block_z = code % 8
    slab = number % slabs
    slot = number // slabs
    data = incoming[slab]
    data = jnp.where(slot == 0, data[0:4], data[4:8])
    shape = (8, data.shape[1])
    x = data[0:1]
    y = data[1:2] - (block_y * YB).astype(jnp.float32)
    z = jnp.broadcast_to(data[2:3] - (block_z * ZB).astype(jnp.float32), shape)
    lane = lax.broadcasted_iota(jnp.int32, (1, shape[1]), 1)
    kind = jnp.broadcast_to(jnp.where(lane < LIVE_LANES, data[3:4], DEAD), shape)
    coef = jnp.zeros(shape, jnp.float32)
    for t in range(table.shape[0]):
        coef = jnp.where(kind == t, table[t], coef)
    high, low = [], []
    for pair in range(3 * ZB // 2):
        parts = [hat(z - (2.0 * pair + i)) * coef for i in range(2)]
        part = jnp.concatenate(parts, axis=0)
        top = part.astype(jnp.bfloat16)
        high.append(top)
        low.append((part - top.astype(jnp.float32)).astype(jnp.bfloat16))
    right = jnp.concatenate(
        [jnp.concatenate(high, axis=0), jnp.concatenate(low, axis=0)], axis=1
    )
    rows = pl.ds(pl.multiple_of(block_y * YB, YB), 3 * YB)
    lanes = pl.ds(pl.multiple_of(block_z * 128, 128), 3 * 128)
    window = cells[:, rows, lanes].reshape(cells.shape[0] * 3 * YB, 3 * 128)
    mixed = jnp.dot(window, right, preferred_element_type=jnp.float32)
    total = jnp.zeros((3 * YB, shape[1]), jnp.float32)
    for i in range(cells.shape[0]):
        part = mixed[i * 3 * YB : (i + 1) * 3 * YB]
        total = total + hat(x - float(i)) * (part[:, : shape[1]] + part[:, shape[1] :])
    level = lax.broadcasted_iota(jnp.int32, total.shape, 0).astype(jnp.float32)
    total = total * hat(y - level)
    out = total[0:8]
    for i in range(1, 3 * YB // 8):
        out = out + total[8 * i : 8 * i + 8]
    sums[number] = out


def score_kernel(tile, incoming, weights, own, left, right, far_a, far_b, out, cells, table, sums, sems):
    tiles = cells.shape[1] // own.shape[1]
    height = own.shape[1]
    half = own.shape[0] // 2
    me = tile[0]

    def place(shift):
        return pl.ds(pl.multiple_of(lax.rem(me + shift, tiles) * height, height), height)

    copies = [
        pltpu.make_async_copy(own, cells.at[:, place(0), :], sems.at[0]),
        pltpu.make_async_copy(left, cells.at[:, place(tiles - 1), :], sems.at[1]),
        pltpu.make_async_copy(right, cells.at[:, place(1), :], sems.at[2]),
        pltpu.make_async_copy(far_a, cells.at[:half, place(2), :], sems.at[3]),
        pltpu.make_async_copy(far_b, cells.at[half:, place(2), :], sems.at[4]),
    ]
    for copy in copies:
        copy.start()
    slabs = incoming.shape[0]
    chans = weights.shape[1]
    atoms = incoming.shape[2]
    spread = jnp.transpose(weights[...])
    for t in range(weights.shape[0]):
        table[t] = jnp.broadcast_to(spread[:, t : t + 1], (chans, atoms))
    sums[...] = jnp.zeros(sums.shape, jnp.float32)
    heads = jnp.concatenate([incoming[:, 3, :], incoming[:, 7, :]], axis=0)
    heads = jnp.transpose(heads)[LIVE_LANES : LIVE_LANES + 8]
    number = lax.broadcasted_iota(jnp.int32, (1, SLOTS * slabs), 1).astype(jnp.float32)
    keys = number * 128.0 + heads[1:2] * 8.0 + heads[2:3]
    keys = jnp.where(heads[0:1] > 0.5, keys, BIG)
    count = jnp.sum(heads[0:1]).astype(jnp.int32)
    spare = float(SLOTS * slabs * 128)

    def draw(keys):
        least = jnp.min(keys)
        keys = jnp.where(keys == least, BIG, keys)
        return keys, jnp.minimum(least, spare).astype(jnp.int32)

    keys, one = draw(keys)
    keys, two = draw(keys)
    for copy in copies:
        copy.wait()

    def step(i, carry):
        keys, one, two = carry
        keys, next_one = draw(keys)
        keys, next_two = draw(keys)
        score_pose(one, incoming, table, cells, sums)
        score_pose(two, incoming, table, cells, sums)
        return keys, next_one, next_two

    lax.fori_loop(0, (count + 1) // 2, step, (keys, one, two))
    lane = lax.broadcasted_iota(jnp.int32, (slabs, atoms), 1)
    result = jnp.zeros((slabs, atoms), jnp.float32)
    for slot in range(SLOTS):
        part = jnp.sum(sums[slot * slabs : (slot + 1) * slabs], axis=1)
        part = jnp.sum(part, axis=1, keepdims=True)
        result = jnp.where(lane == slot, part, result)
    out[...] = result


def scored(grid, type_table, counts, types, offsets, route, base_y, base_z):
    slabs = lax.axis_size("slab")
    tiles = lax.axis_size("tile")
    cells_x, cells_y, wide_z = grid.shape
    poses, atoms = types.shape
    chans = type_table.shape[1]
    half = cells_x // 2
    up = [(i, (i + 1) % tiles) for i in range(tiles)]
    down = [(i, (i - 1) % tiles) for i in range(tiles)]
    left = lax.ppermute(grid, "tile", up)
    right = lax.ppermute(grid, "tile", down)
    far_a = lax.ppermute(left[:half], "tile", up)
    far_b = lax.ppermute(right[half:], "tile", down)
    tile = lax.axis_index("tile").astype(jnp.int32).reshape(1)
    outgoing, spot = pl.pallas_call(
        lambda *refs: send_kernel(*refs, span_x=float(cells_x - 1)),
        out_shape=(
            jax.ShapeDtypeStruct((slabs, 8, atoms), jnp.float32),
            jax.ShapeDtypeStruct((poses,), jnp.int32),
        ),
        in_specs=[smem(), smem(), smem(), smem(), smem(), vmem(), vmem()],
        out_specs=(vmem(), smem()),
        scratch_shapes=[pltpu.SMEM((slabs,), jnp.int32)],
        name="send",
    )(tile, route, counts, base_y, base_z, types, offsets)
    incoming = lax.all_to_all(outgoing, "slab", split_axis=0, concat_axis=0, tiled=True)
    partial = pl.pallas_call(
        score_kernel,
        out_shape=jax.ShapeDtypeStruct((slabs, atoms), jnp.float32),
        in_specs=[smem(), vmem(), vmem(), hbm(), hbm(), hbm(), hbm(), hbm()],
        out_specs=vmem(),
        scratch_shapes=[
            pltpu.VMEM((cells_x, tiles * cells_y, wide_z), jnp.bfloat16),
            pltpu.VMEM((type_table.shape[0], chans, atoms), jnp.float32),
            pltpu.VMEM((SLOTS * slabs + 1, 8, atoms), jnp.float32),
            pltpu.SemaphoreType.DMA((5,)),
        ],
        compiler_params=pltpu.CompilerParams(vmem_limit_bytes=32 << 20),
        cost_estimate=pl.CostEstimate(
            flops=4000000000, bytes_accessed=8 << 20, transcendentals=0
        ),
        name="score",
    )(tile, incoming, type_table, grid, left, right, far_a, far_b)
    returned = lax.all_to_all(partial, "slab", split_axis=0, concat_axis=0, tiled=True)
    flat = returned[:, :SLOTS].reshape(1, slabs * SLOTS)
    hits = spot[:, None] == jnp.arange(slabs * SLOTS, dtype=jnp.int32)[None, :]
    energy = jnp.sum(jnp.where(hits, flat, 0.0), axis=1)
    return energy / counts.astype(jnp.float32)


def solution(mesh):
    in_specs = (
        P("slab", "tile", None),
        P(),
        P(("slab", "tile")),
        P(("slab", "tile"), None),
        P(("slab", "tile"), None, None),
        P("slab", None),
        P(("slab", "tile")),
        P(("slab", "tile")),
    )
    out_specs = P(("slab", "tile"))
    return jax.shard_map(scored, mesh=mesh, in_specs=in_specs, out_specs=out_specs, check_vma=False)
```

time: 249 us -> 87.6 us (0.35)
  local copies, waits for them, and re-layouts: 176 us -> 4.35 us
  waiting for transfers between devices: 10.2 us -> 32.8 us
  other arithmetic: 21.6 us -> 0.7 us
  blocking collectives: 8.23 us -> 20.1 us
  starting transfers between devices: 29.9 us -> 21.8 us
  Pallas kernels: 0 us -> 7.45 us
    gather x7 -> x0, local copies, waits for them, and re-layouts: 136 us -> none  [the longest x4 133 us: score(): values = jnp.take(table, index + step_x * lines, axis=0).astype(jnp.float32)]
    reshape x4 -> x0, local copies, waits for them, and re-layouts: 22.3 us -> none  [the longest x2 22 us: corner_table(): return square.reshape(cells_x * cells_y * (cells_z - 1), 4 * chans)]
    ppermute x1 -> x4, waiting for transfers between devices: 0.94 us -> 20.9 us  [the longest x1 20.9 us: scored(): left = lax.ppermute(grid, 'tile', up)]
    all_to_all x3 -> x1, starting transfers between devices: 28.6 us -> 15.1 us  [scored(): lax.all_to_all(outgoing, 'slab', split_axis=0, concat_axis=0, tiled=True)]
    all_to_all x1, blocking collectives: 8.23 us -> 20.1 us  [scored(): lax.all_to_all(partial, 'slab', split_axis=0, concat_axis=0, tiled=True)]
    concatenate x3 -> x0, local copies, waits for them, and re-layouts: 11.8 us -> none  [the longest x1 10 us: corner_table(): square = jnp.concatenate([paired[:, :-1], paired[:, 1:]], axis=3)]
    concatenate x4 -> x0, other arithmetic: 8.62 us -> none  [the longest x1 6.22 us: corner_table(): square = jnp.concatenate([paired[:, :-1], paired[:, 1:]], axis=3)]
    pallas_call x0 -> x2, Pallas kernels: none -> 7.45 us  [the longest x1 4.88 us: scored(): pl.pallas_call(score_kernel, out_shape=jax.ShapeDtypeStruct((slabs, atoms...]
  transfers between devices with their start and end apart: 4 -> 5, of which waited for: 2 -> 2; matrix products, arithmetic and copies ran while one was open for 19% -> 4% of each run, Pallas kernels for 0% -> 0%
where the time goes in v1:
time: 87.6 us; the launch traced here: 87.2 us
  waiting for transfers between devices  32.8 us (37%)
  starting transfers between devices  21.8 us (25%)
  blocking collectives  20.1 us (23%)
  Pallas kernels  7.45 us (9%)
  local copies, waits for them, and re-layouts  4.35 us (5%)
    ppermute x1, waiting for transfers between devices, scored(): left = lax.ppermute(grid, 'tile', up)  20.9 us
    all_to_all x1, blocking collectives, scored(): lax.all_to_all(partial, 'slab', split_axis=0, concat_axis=0, tiled=True)  20.1 us
    all_to_all x1, starting transfers between devices, scored(): lax.all_to_all(outgoing, 'slab', split_axis=0, concat_axis=0, tiled=True)  15.1 us
    all_to_all x1, waiting for transfers between devices, scored(): lax.all_to_all(outgoing, 'slab', split_axis=0, concat_axis=0, tiled=True)  11.9 us
    pallas_call x1, Pallas kernels, scored(): pl.pallas_call(score_kernel, out_shape=jax.ShapeDtypeStruct((slabs, atoms...  4.88 us
    pallas_call x1, Pallas kernels, scored(): pl.pallas_call(lambda *refs: send_kernel(*refs, span_x=float(cells_x - 1)...  2.57 us
    unnamed x15, local copies, waits for them, and re-layouts  2.57 us
    ppermute x1, starting transfers between devices, scored(): left = lax.ppermute(grid, 'tile', up)  2.03 us
  transfers between devices with their start and end apart: 5, of which 2 were waited for; matrix products, arithmetic and copies ran while one was open for 4% of the time, Pallas kernels for 0%

profile of v1, /device:TPU:1, one launch (start us, length us, event | category | flops | bytes accessed | tf_op | source)
XLA Modules:
  0.0 87.2 jit_solution(7116723458981275981)
XLA Ops:
  0.0 2.0 %collective-permute-start = (bf16[8,64,1024]{2,1,0:T(8,128)(2,1)}, bf16[8,64,1024]{2,1,0:T(8,128)(2,1)S(1)}, u32[]{:S(2)}, u32[]{:S(2)}) collective-permute-start(bf16[8,64,1024]{2,1,0:T(8,128)(2,1)} %own.1), channel_id=1, source_target_pairs={{0,1},{1,2},{2,3},{3,0},{4,5},{5,6},{6,7},{7,4},{8,9},{9,10},{10,1... | collective-permute-start | bytes 3145736 | tf_op jit(solution)/shard_map/ppermute | solution.py:178
  2.0 1.3 %collective-permute-start.1 = (bf16[8,64,1024]{2,1,0:T(8,128)(2,1)}, bf16[8,64,1024]{2,1,0:T(8,128)(2,1)S(1)}, u32[]{:S(2)}, u32[]{:S(2)}) collective-permute-start(bf16[8,64,1024]{2,1,0:T(8,128)(2,1)} %own.1), channel_id=1, source_target_pairs={{0,3},{1,0},{2,1},{3,2},{4,7},{5,4},{6,5},{7,6},{8,11},{9,8},{10,9... | collective-permute-start | bytes 3145736 | tf_op jit(solution)/shard_map/ppermute | solution.py:179
  3.3 20.9 %collective-permute-done.left = bf16[8,64,1024]{2,1,0:T(8,128)(2,1)S(1)} collective-permute-done((bf16[8,64,1024]{2,1,0:T(8,128)(2,1)}, bf16[8,64,1024]{2,1,0:T(8,128)(2,1)S(1)}, u32[]{:S(2)}, u32[]{:S(2)}) %collective-permute-start) | collective-permute-done | bytes 1048608 | tf_op jit(solution)/shard_map/ppermute | solution.py:178
  24.2 0.8 slice.12
  25.0 0.0 copy-start
  25.0 1.9 %collective-permute-start.2 = (bf16[4,64,1024]{2,1,0:T(8,128)(2,1)}, bf16[4,64,1024]{2,1,0:T(8,128)(2,1)}, u32[]{:S(2)}, u32[]{:S(2)}) collective-permute-start(bf16[4,64,1024]{2,1,0:T(8,128)(2,1)} %slice.12), channel_id=1, source_target_pairs={{0,1},{1,2},{2,3},{3,0},{4,5},{5,6},{6,7},{7,4},{8,9},{9,10},{10,1... | collective-permute-start | bytes 1572872 | tf_op jit(solution)/shard_map/ppermute | solution.py:180
  26.9 0.0 collective-permute-done.1.right
  26.9 0.0 copy-start.3
  26.9 0.8 slice.13
  27.7 0.0 copy-start.1
  27.7 1.5 %collective-permute-start.3 = (bf16[4,64,1024]{2,1,0:T(8,128)(2,1)}, bf16[4,64,1024]{2,1,0:T(8,128)(2,1)}, u32[]{:S(2)}, u32[]{:S(2)}) collective-permute-start(bf16[4,64,1024]{2,1,0:T(8,128)(2,1)} %slice.13), channel_id=1, source_target_pairs={{0,3},{1,0},{2,1},{3,2},{4,7},{5,4},{6,5},{7,6},{8,11},{9,8},{10,9... | collective-permute-start | bytes 1572872 | tf_op jit(solution)/shard_map/ppermute | solution.py:181
  29.2 0.0 copy-done.3
  29.2 0.7 copy.19.refs_1_
  29.9 0.0 copy-done.1
  29.9 0.6 copy.20.refs_6_
  30.6 2.6 %send.1 = (f32[64,8,128]{2,1,0:T(8,128)}, s32[16]{0:T(128)}) custom-call(s32[1]{0:T(128)} %bitcast.refs_0_.tile, s32[64,1]{1,0:T(8,128)} %copy.19.refs_1_, s32[16]{0:T(128)} %refs_2_.1, s32[16]{0:T(128)} %refs_3_.1, s32[16]{0:T(128)} %refs_4_.1, s32[16,128]{1,0:T(8,128)} %refs_5_.1, f32[16,3,128]{2,1,0:T(4,128)} %copy.20.refs_6_), custom_call_target="tpu_custom_call" | custom-call | tf_op jit(solution)/shard_map/send/pallas_call | solution.py:183
  33.1 0.0 copy-start.2
  33.2 15.1 %all-to-all-start = ((f32[64,8,128]{2,1,0:T(8,128)}), f32[64,8,128]{2,1,0:T(8,128)S(1)}, u32[]{:S(2)}, u32[]{:S(2)}) async-start(f32[64,8,128]{2,1,0:T(8,128)} %get-tuple-element.8), calls=%async_computation | async-start | bytes 524288 | tf_op jit(solution)/shard_map/all_to_all | solution.py:194
  48.3 0.0 copy-done.2
  48.3 0.1 copy.21.weights
  48.4 11.9 %all-to-all-done.incoming = f32[64,8,128]{2,1,0:T(8,128)S(1)} async-done(((f32[64,8,128]{2,1,0:T(8,128)}), f32[64,8,128]{2,1,0:T(8,128)S(1)}, u32[]{:S(2)}, u32[]{:S(2)}) %all-to-all-start) | async-done | bytes 262176 | tf_op jit(solution)/shard_map/all_to_all | solution.py:194
  60.3 0.0 collective-permute-done.2.far_a
  60.3 0.0 collective-permute-done.3.far_b
  60.3 0.0 copy-done
  60.3 4.9 %score.1 = f32[64,128]{1,0:T(8,128)S(1)} custom-call(s32[1]{0:T(128)} %bitcast.refs_0_.tile, f32[64,8,128]{2,1,0:T(8,128)S(1)} %all-to-all-done.incoming, f32[16,8]{1,0:T(8,128)S(1)} %copy.21.weights, bf16[8,64,1024]{2,1,0:T(8,128)(2,1)S(1)} %copy-done, bf16[8,64,1024]{2,1,0:T(8,128)(2,1)S(1)} %collective-permute-done.left, ...), custom_call_target="tpu_custom_call" | custom-call | flops 4000000000 | bytes 8388608 | tf_op jit(solution)/shard_map/score/pallas_call | solution.py:195
  65.2 20.1 %all_to_all.17 = f32[64,1,128]{2,1,0:T(1,128)S(1)} all-to-all(f32[64,1,128]{2,1,0:T(1,128)S(1)} %bitcast.6), channel_id=1, replica_groups=mesh['slab'=64,'tile'=4] {'slab'}, dimensions={0} | all-to-all | bytes 65536 | tf_op jit(solution)/shard_map/all_to_all | solution.py:212
  85.2 0.1 broadcast_in_dim.16
  85.4 0.0 copy-start.5
  85.4 0.7 copy-done.5
  86.0 0.0 copy-start.4
  86.0 0.2 select_reduce_fusion
  86.2 0.5 copy-done.4
  86.7 0.5 convert_divide_fusion
Async XLA Ops:
  0.0 24.2 %collective-permute-start = (bf16[8,64,1024]{2,1,0:T(8,128)(2,1)}, bf16[8,64,1024]{2,1,0:T(8,128)(2,1)S(1)}, u32[]{:S(2)}, u32[]{:S(2)}) collective-permute-start(bf16[8,64,1024]{2,1,0:T(8,128)(2,1)} %own.1), channel_id=1, source_target_pairs={{0,1},{1,2},{2,3},{3,0},{4,5},{5,6},{6,7},{7,4},{8,9},{9,10},{10,1... | collective-permute-start | bytes 3145736 | tf_op jit(solution)/shard_map/ppermute | solution.py:178
  2.0 24.9 %collective-permute-start.1 = (bf16[8,64,1024]{2,1,0:T(8,128)(2,1)}, bf16[8,64,1024]{2,1,0:T(8,128)(2,1)S(1)}, u32[]{:S(2)}, u32[]{:S(2)}) collective-permute-start(bf16[8,64,1024]{2,1,0:T(8,128)(2,1)} %own.1), channel_id=1, source_target_pairs={{0,3},{1,0},{2,1},{3,2},{4,7},{5,4},{6,5},{7,6},{8,11},{9,8},{10,9... | collective-permute-start | bytes 3145736 | tf_op jit(solution)/shard_map/ppermute | solution.py:179
  25.0 35.3 %copy-start = (bf16[8,64,1024]{2,1,0:T(8,128)(2,1)S(1)}, bf16[8,64,1024]{2,1,0:T(8,128)(2,1)}, u32[]{:S(2)}) copy-start(bf16[8,64,1024]{2,1,0:T(8,128)(2,1)} %own.1) | copy-start | bytes 3145732
  25.0 35.3 %collective-permute-start.2 = (bf16[4,64,1024]{2,1,0:T(8,128)(2,1)}, bf16[4,64,1024]{2,1,0:T(8,128)(2,1)}, u32[]{:S(2)}, u32[]{:S(2)}) collective-permute-start(bf16[4,64,1024]{2,1,0:T(8,128)(2,1)} %slice.12), channel_id=1, source_target_pairs={{0,1},{1,2},{2,3},{3,0},{4,5},{5,6},{6,7},{7,4},{8,9},{9,10},{10,1... | collective-permute-start | bytes 1572872 | tf_op jit(solution)/shard_map/ppermute | solution.py:180
  26.9 2.3 %copy-start.3 = (s32[64,1]{0,1:T(1,128)S(1)}, s32[64,1]{0,1:T(1,128)}, u32[]{:S(2)}) copy-start(s32[64,1]{0,1:T(1,128)} %param.13) | copy-start | bytes 772
  27.7 2.2 %copy-start.1 = (f32[16,3,128]{2,0,1:T(8,128)S(1)}, f32[16,3,128]{2,0,1:T(8,128)}, u32[]{:S(2)}) copy-start(f32[16,3,128]{2,0,1:T(8,128)} %param.12) | copy-start | bytes 73732
  27.7 32.6 %collective-permute-start.3 = (bf16[4,64,1024]{2,1,0:T(8,128)(2,1)}, bf16[4,64,1024]{2,1,0:T(8,128)(2,1)}, u32[]{:S(2)}, u32[]{:S(2)}) collective-permute-start(bf16[4,64,1024]{2,1,0:T(8,128)(2,1)} %slice.13), channel_id=1, source_target_pairs={{0,3},{1,0},{2,1},{3,2},{4,7},{5,4},{6,5},{7,6},{8,11},{9,8},{10,9... | collective-permute-start | bytes 1572872 | tf_op jit(solution)/shard_map/ppermute | solution.py:181
  33.1 15.2 %copy-start.2 = (f32[16,8]{0,1:T(8,128)S(1)}, f32[16,8]{0,1:T(8,128)}, u32[]{:S(2)}) copy-start(f32[16,8]{0,1:T(8,128)} %param.9) | copy-start | bytes 1540
  33.2 27.1 %all-to-all-start = ((f32[64,8,128]{2,1,0:T(8,128)}), f32[64,8,128]{2,1,0:T(8,128)S(1)}, u32[]{:S(2)}, u32[]{:S(2)}) async-start(f32[64,8,128]{2,1,0:T(8,128)} %get-tuple-element.8), calls=%async_computation | async-start | bytes 524288 | tf_op jit(solution)/shard_map/all_to_all | solution.py:194
  85.4 0.7 copy-start.5
  86.0 0.7 copy-start.4

commit v2 on v1

v2 whole, which is shorter than its diff:
```python
import functools
import jax
import jax.numpy as jnp
from jax import lax
from jax.experimental import pallas as pl
from jax.experimental.pallas import tpu as pltpu
from jax.sharding import PartitionSpec as P

SPAN = 32
SLOTS = 2
YB = 16
ZB = 16
NB = 3
LIVE_LANES = 120
DEAD = 99.0
BIG = 1.0e6


def smem():
    return pl.BlockSpec(memory_space=pltpu.SMEM)


def vmem():
    return pl.BlockSpec(memory_space=pltpu.VMEM)


def hbm():
    return pl.BlockSpec(memory_space=pl.ANY)


def send_kernel(tile, route, counts, base_y, base_z, types, offsets, out, pick, used, *, span_x):
    poses, atoms = types.shape
    slabs = out.shape[0]
    out[...] = jnp.zeros(out.shape, jnp.float32)

    def clear(i, carry):
        used[i] = 0
        return carry

    lax.fori_loop(0, slabs, clear, 0)
    lane = lax.broadcasted_iota(jnp.int32, (1, atoms), 1)
    row = lax.broadcasted_iota(jnp.int32, (8, atoms), 0)
    first = tile[0] * poses
    for p in range(poses):
        slab = route[first + p]
        slot = used[slab]
        used[slab] = slot + 1
        count = jnp.broadcast_to(counts[p].astype(jnp.float32), (1, atoms))
        pick[p : p + 1] = jnp.where(lane == SLOTS * slab + slot, 1.0 / count, 0.0)
        x = offsets[0, p : p + 1] * span_x
        y = base_y[p].astype(jnp.float32) + offsets[1, p : p + 1] * SPAN
        z = base_z[p].astype(jnp.float32) + offsets[2, p : p + 1] * SPAN
        kind = jnp.where(lane < counts[p], types[p : p + 1].astype(jnp.float32), DEAD)
        kind = jnp.where(lane == LIVE_LANES, 1.0, kind)
        kind = jnp.where(lane == LIVE_LANES + 1, (base_y[p] // YB).astype(jnp.float32), kind)
        kind = jnp.where(lane == LIVE_LANES + 2, (base_z[p] // ZB).astype(jnp.float32), kind)
        block = jnp.concatenate([x, y, z, kind, x, y, z, kind], axis=0)
        out[slab] = jnp.where(row // 4 == slot, block, out[slab])


def hat(distance):
    return jnp.maximum(1.0 - jnp.abs(distance), 0.0)


def split_key(key, slabs):
    number = key // 128
    code = key % 128
    return number, number % slabs, number // slabs, code // 8, code % 8


def build(key, incoming, table, hats, right):
    _, slab, slot, _, block_z = split_key(key, incoming.shape[0])
    data = incoming[slab]
    data = jnp.where(slot == 0, data[0:4], data[4:8])
    atoms = data.shape[1]
    lane = lax.broadcasted_iota(jnp.int32, (1, atoms), 1)
    level = lax.broadcasted_iota(jnp.int32, (NB * ZB, atoms), 0).astype(jnp.float32)
    hats[...] = hat(data[2:3] - (block_z * ZB).astype(jnp.float32) - level)
    shape = (table.shape[1], atoms)
    kind = jnp.broadcast_to(jnp.where(lane < LIVE_LANES, data[3:4], DEAD), shape)
    coef = jnp.zeros(shape, jnp.float32)
    for t in range(table.shape[0]):
        coef = jnp.where(kind == t, table[t], coef)
    for pair in range(NB * ZB // 2):
        parts = [
            jnp.broadcast_to(hats[2 * pair + i : 2 * pair + i + 1], shape) * coef
            for i in range(2)
        ]
        part = jnp.concatenate(parts, axis=0)
        top = part.astype(jnp.bfloat16)
        rows = slice(2 * pair * shape[0], 2 * (pair + 1) * shape[0])
        right[rows, :atoms] = top
        right[rows, atoms:] = (part - top.astype(jnp.float32)).astype(jnp.bfloat16)


def apply(key, incoming, window, start_y, right, hats, sums):
    number, slab, slot, _, _ = split_key(key, incoming.shape[0])
    data = incoming[slab]
    data = jnp.where(slot == 0, data[0:4], data[4:8])
    atoms = data.shape[1]
    wide = window.shape[0]
    mixed = jnp.dot(
        window.reshape(wide * NB * YB, window.shape[2]),
        right[...],
        preferred_element_type=jnp.float32,
    )
    level = lax.broadcasted_iota(jnp.int32, (wide, atoms), 0).astype(jnp.float32)
    hats[...] = hat(data[0:1] - level)
    total = None
    for i in range(wide):
        part = mixed[i * NB * YB : (i + 1) * NB * YB]
        part = hats[i : i + 1] * (part[:, :atoms] + part[:, atoms:])
        total = part if total is None else total + part
    level = lax.broadcasted_iota(jnp.int32, total.shape, 0).astype(jnp.float32)
    total = total * hat(data[1:2] - start_y.astype(jnp.float32) - level)
    out = total[0:8]
    for i in range(1, NB * YB // 8):
        out = out + total[8 * i : 8 * i + 8]
    sums[number] = out


def score(incoming, weights, wanted, window_of, table, sums, tools):
    slabs, _, atoms = incoming.shape
    z_hats, x_hats, rights = tools
    chans = weights.shape[0]
    for t in range(weights.shape[1]):
        table[t] = jnp.broadcast_to(weights[:, t : t + 1], (chans, atoms))
    sums[...] = jnp.zeros(sums.shape, jnp.float32)
    heads = jnp.concatenate([incoming[:, 3, :], incoming[:, 7, :]], axis=0)
    heads = jnp.transpose(heads)[LIVE_LANES : LIVE_LANES + 8]
    number = lax.broadcasted_iota(jnp.int32, (1, SLOTS * slabs), 1).astype(jnp.float32)
    keys = number * 128.0 + heads[1:2] * 8.0 + heads[2:3]
    live = (heads[0:1] > 0.5) & wanted(heads[1:2])
    keys = jnp.where(live, keys, BIG)
    count = jnp.sum(jnp.where(live, 1.0, 0.0)).astype(jnp.int32)
    spare = float(SLOTS * slabs * 128)

    def draw(keys):
        least = jnp.min(keys)
        keys = jnp.where(keys == least, BIG, keys)
        return keys, jnp.minimum(least, spare).astype(jnp.int32)

    def put(key, i):
        build(key, incoming, table, z_hats[i], rights[i])

    def use(key, i):
        _, _, _, block_y, block_z = split_key(key, slabs)
        lanes = pl.ds(pl.multiple_of(block_z * 128, 128), NB * 128)
        window, start_y = window_of(block_y, lanes)
        apply(key, incoming, window, start_y, rights[i], x_hats[i], sums)

    keys, one = draw(keys)
    keys, two = draw(keys)
    put(one, 0)

    def step(i, carry):
        keys, one, two = carry
        keys, three = draw(keys)
        keys, four = draw(keys)
        use(one, 0)
        put(two, 1)
        use(two, 1)
        put(three, 0)
        return keys, three, four

    lax.fori_loop(0, (count + 1) // 2, step, (keys, one, two))
    lane = lax.broadcasted_iota(jnp.int32, (slabs, atoms), 1)
    result = jnp.zeros((slabs, atoms), jnp.float32)
    for slot in range(SLOTS):
        part = jnp.sum(sums[slot * slabs : (slot + 1) * slabs], axis=1)
        part = jnp.sum(part, axis=1, keepdims=True)
        result = jnp.where(lane == slot, part, result)
    return result


def tile_of(block, per_tile):
    return jnp.floor((block + 0.5) / per_tile)


def near_kernel(tile, incoming, weights, own, left_a, left_b, right_a, right_b, out, cells, sems, table, sums, *tools):
    height = own.shape[1]
    tiles = cells.shape[1] // height
    half = left_a.shape[0]
    me = tile[0]

    def place(shift):
        return pl.ds(pl.multiple_of(lax.rem(me + shift, tiles) * height, height), height)

    copies = [
        pltpu.make_async_copy(own, cells.at[:, place(0), :], sems.at[0]),
        pltpu.make_async_copy(left_a, cells.at[:half, place(tiles - 1), :], sems.at[1]),
        pltpu.make_async_copy(left_b, cells.at[half:, place(tiles - 1), :], sems.at[2]),
        pltpu.make_async_copy(right_a, cells.at[:half, place(1), :], sems.at[3]),
        pltpu.make_async_copy(right_b, cells.at[half:, place(1), :], sems.at[4]),
    ]
    for copy in copies:
        copy.start()
    cells[:, place(2), :] = jnp.zeros(own.shape, cells.dtype)
    far = lax.rem(me + 2, tiles).astype(jnp.float32)
    for copy in copies:
        copy.wait()

    def wanted(block):
        per = height // YB
        return (tile_of(block, per) != far) | (tile_of(block + (NB - 1), per) != far)

    def window_of(block, lanes):
        start = block * YB
        return cells[:, pl.ds(pl.multiple_of(start, YB), NB * YB), lanes], start

    out[...] = score(incoming, weights, wanted, window_of, table, sums, (tools[0:2], tools[2:4], tools[4:6]))


def far_kernel(tile, incoming, weights, near, far_a, far_b, out, table, sums, *tools, tiles):
    height = far_a.shape[1]
    per = height // YB
    far = lax.rem(tile[0] + 2, tiles)
    far_f = far.astype(jnp.float32)

    def wanted(block):
        return (tile_of(block, per) == far_f) | (tile_of(block + (NB - 1), per) == far_f)

    def window_of(block, lanes):
        start = jnp.clip(block - per * far, 0, per - NB) * YB
        rows = pl.ds(pl.multiple_of(start, YB), NB * YB)
        window = jnp.concatenate([far_a[:, rows, lanes], far_b[:, rows, lanes]], axis=0)
        return window, start + far * height

    more = score(incoming, weights, wanted, window_of, table, sums, (tools[0:2], tools[2:4], tools[4:6]))
    out[...] = near[...] + more


def scored(grid, type_table, counts, types, offsets, route, base_y, base_z):
    slabs = lax.axis_size("slab")
    tiles = lax.axis_size("tile")
    cells_x, cells_y, wide_z = grid.shape
    poses, atoms = types.shape
    kinds, chans = type_table.shape
    half = cells_x // 2
    up = [(i, (i + 1) % tiles) for i in range(tiles)]
    down = [(i, (i - 1) % tiles) for i in range(tiles)]
    left_a = lax.ppermute(grid[:half], "tile", up)
    right_b = lax.ppermute(grid[half:], "tile", down)
    left_b = lax.ppermute(grid[half:], "tile", up)
    right_a = lax.ppermute(grid[:half], "tile", down)
    far_a = lax.ppermute(left_a, "tile", up)
    far_b = lax.ppermute(right_b, "tile", down)
    tile = lax.axis_index("tile").astype(jnp.int32).reshape(1)
    outgoing, pick = pl.pallas_call(
        functools.partial(send_kernel, span_x=float(cells_x - 1)),
        out_shape=(
            jax.ShapeDtypeStruct((slabs, 8, atoms), jnp.float32),
            jax.ShapeDtypeStruct((poses, atoms), jnp.float32),
        ),
        in_specs=[smem(), smem(), smem(), smem(), smem(), vmem(), vmem()],
        out_specs=(vmem(), vmem()),
        scratch_shapes=[pltpu.SMEM((slabs,), jnp.int32)],
        name="send",
    )(tile, route.reshape(-1), counts, base_y, base_z, types, jnp.swapaxes(offsets, 0, 1))
    incoming = lax.all_to_all(outgoing, "slab", split_axis=0, concat_axis=0, tiled=True)
    weights = jnp.swapaxes(type_table, 0, 1)
    result = jax.ShapeDtypeStruct((slabs, atoms), jnp.float32)
    shared = [
        pltpu.VMEM((kinds, chans, atoms), jnp.float32),
        pltpu.VMEM((SLOTS * slabs + 1, 8, atoms), jnp.float32),
        pltpu.VMEM((NB * ZB, atoms), jnp.float32),
        pltpu.VMEM((NB * ZB, atoms), jnp.float32),
        pltpu.VMEM((cells_x, atoms), jnp.float32),
        pltpu.VMEM((cells_x, atoms), jnp.float32),
        pltpu.VMEM((NB * ZB * chans, 2 * atoms), jnp.bfloat16),
        pltpu.VMEM((NB * ZB * chans, 2 * atoms), jnp.bfloat16),
    ]
    near = pl.pallas_call(
        near_kernel,
        out_shape=result,
        in_specs=[smem(), vmem(), vmem()] + [hbm()] * 5,
        out_specs=vmem(),
        scratch_shapes=[
            pltpu.VMEM((cells_x, tiles * cells_y, wide_z), jnp.bfloat16),
            pltpu.SemaphoreType.DMA((5,)),
        ]
        + shared,
        compiler_params=pltpu.CompilerParams(vmem_limit_bytes=32 << 20),
        cost_estimate=pl.CostEstimate(
            flops=4000000000, bytes_accessed=6 << 20, transcendentals=0
        ),
        name="near",
    )(tile, incoming, weights, grid, left_a, left_b, right_a, right_b)
    partial = pl.pallas_call(
        functools.partial(far_kernel, tiles=tiles),
        out_shape=result,
        in_specs=[smem()] + [vmem()] * 5,
        out_specs=vmem(),
        scratch_shapes=shared,
        compiler_params=pltpu.CompilerParams(vmem_limit_bytes=32 << 20),
        cost_estimate=pl.CostEstimate(
            flops=1000000000, bytes_accessed=2 << 20, transcendentals=0
        ),
        name="far",
    )(tile, incoming, weights, near, far_a, far_b)
    returned = lax.all_to_all(partial, "slab", split_axis=0, concat_axis=0, tiled=True)
    flat = returned[:, :SLOTS].reshape(1, slabs * SLOTS)
    return jnp.sum(flat * pick, axis=1)


def solution(mesh):
    in_specs = (
        P("slab", "tile", None),
        P(),
        P(("slab", "tile")),
        P(("slab", "tile"), None),
        P(("slab", "tile"), None, None),
        P("slab", None),
        P(("slab", "tile")),
        P(("slab", "tile")),
    )
    out_specs = P(("slab", "tile"))
    return jax.shard_map(scored, mesh=mesh, in_specs=in_specs, out_specs=out_specs, check_vma=False)
```

time: 87.6 us -> 68.6 us (0.78)
  waiting for transfers between devices: 32.8 us -> 9.21 us
  blocking collectives: 20.1 us -> 24.1 us
  local copies, waits for them, and re-layouts: 4.35 us -> 3.03 us
  Pallas kernels: 7.45 us -> 8.76 us
    ppermute x4 -> x6, waiting for transfers between devices: 20.9 us -> 0.02 us  [the longest x1 0.01 us: scored(): left_a = lax.ppermute(grid[:half], 'tile', up)]
    all_to_all x1, blocking collectives: 20.1 us -> 24.1 us  [scored(): lax.all_to_all(partial, 'slab', split_axis=0, concat_axis=0, tiled=True)]
    all_to_all x1, waiting for transfers between devices: 11.9 us -> 9.2 us  [scored(): lax.all_to_all(outgoing, 'slab', split_axis=0, concat_axis=0, tiled=True)]
    ppermute x4 -> x6, starting transfers between devices: 6.68 us -> 8.71 us  [the longest x1 2.66 us: scored(): far_b = lax.ppermute(right_b, 'tile', down)]
    unnamed x15 -> x6, local copies, waits for them, and re-layouts: 2.57 us -> 0.57 us
    all_to_all x1, starting transfers between devices: 15.1 us -> 13.8 us  [scored(): lax.all_to_all(outgoing, 'slab', split_axis=0, concat_axis=0, tiled=True)]
    pallas_call x2 -> x3, Pallas kernels: 7.45 us -> 8.76 us  [the longest x1 3.55 us: scored(): pl.pallas_call(near_kernel, out_shape=result, in_specs=[smem(), vmem(), v...]
    slice x2 -> x1, local copies, waits for them, and re-layouts: 1.65 us -> 2.33 us  [scored(): left_b = lax.ppermute(grid[half:], 'tile', up)]
  transfers between devices with their start and end apart: 5 -> 7, of which waited for: 2 -> 1; matrix products, arithmetic and copies ran while one was open for 4% -> 0% of each run, Pallas kernels for 0% -> 5%
where the time goes in v2:
time: 68.6 us; the launch traced here: 68.3 us
  blocking collectives  24.1 us (35%)
  starting transfers between devices  22.5 us (33%)
  waiting for transfers between devices  9.21 us (13%)
  Pallas kernels  8.76 us (13%)
  local copies, waits for them, and re-layouts  3.03 us (4%)
    all_to_all x1, blocking collectives, scored(): lax.all_to_all(partial, 'slab', split_axis=0, concat_axis=0, tiled=True)  24.1 us
    all_to_all x1, starting transfers between devices, scored(): lax.all_to_all(outgoing, 'slab', split_axis=0, concat_axis=0, tiled=True)  13.8 us
    all_to_all x1, waiting for transfers between devices, scored(): lax.all_to_all(outgoing, 'slab', split_axis=0, concat_axis=0, tiled=True)  9.2 us
    pallas_call x1, Pallas kernels, scored(): pl.pallas_call(near_kernel, out_shape=result, in_specs=[smem(), vmem(), v...  3.55 us
    pallas_call x1, Pallas kernels, scored(): pl.pallas_call(functools.partial(far_kernel, tiles=tiles), out_shape=resu...  3.11 us
    ppermute x1, starting transfers between devices, scored(): far_b = lax.ppermute(right_b, 'tile', down)  2.66 us
    ppermute x1, starting transfers between devices, scored(): right_a = lax.ppermute(grid[:half], 'tile', down)  2.48 us
    slice x1, local copies, waits for them, and re-layouts, scored(): left_b = lax.ppermute(grid[half:], 'tile', up)  2.33 us
  transfers between devices with their start and end apart: 7, of which 1 were waited for; matrix products, arithmetic and copies ran while one was open for 0% of the time, Pallas kernels for 5%

profile of v2, /device:TPU:1, one launch (start us, length us, event | category | flops | bytes accessed | tf_op | source)
XLA Modules:
  0.0 68.3 jit_solution(16569323632219966961)
XLA Ops:
  0.0 0.0 copy-start
  0.0 2.3 %fusion = (bf16[4,64,1024]{2,1,0:T(8,128)(2,1)}, bf16[4,64,1024]{2,1,0:T(8,128)(2,1)}) fusion(bf16[8,64,1024]{2,1,0:T(8,128)(2,1)} %own.1), kind=kLoop, calls=%fused_computation.1 | loop fusion | bytes 2097152 | tf_op jit(solution)/shard_map/slice | solution.py:244
  2.3 2.0 %collective-permute-start = (bf16[4,64,1024]{2,1,0:T(8,128)(2,1)}, bf16[4,64,1024]{2,1,0:T(8,128)(2,1)S(1)}, u32[]{:S(2)}, u32[]{:S(2)}) collective-permute-start(bf16[4,64,1024]{2,1,0:T(8,128)(2,1)} %get-tuple-element.10), channel_id=1, source_target_pairs={{0,1},{1,2},{2,3},{3,0},{4,5},{5,6},{6,7},{7,4},{8,9},{9,10},{10,1... | collective-permute-start | bytes 1572872 | tf_op jit(solution)/shard_map/ppermute | solution.py:242
  4.4 1.3 %collective-permute-start.3 = (bf16[4,64,1024]{2,1,0:T(8,128)(2,1)}, bf16[4,64,1024]{2,1,0:T(8,128)(2,1)S(1)}, u32[]{:S(2)}, u32[]{:S(2)}) collective-permute-start(bf16[4,64,1024]{2,1,0:T(8,128)(2,1)} %get-tuple-element.9), channel_id=1, source_target_pairs={{0,3},{1,0},{2,1},{3,2},{4,7},{5,4},{6,5},{7,6},{8,11},{9,8},{10,9... | collective-permute-start | bytes 1572872 | tf_op jit(solution)/shard_map/ppermute | solution.py:243
  5.6 0.2 collective-permute-start.1
  5.8 2.5 %collective-permute-start.2 = (bf16[4,64,1024]{2,1,0:T(8,128)(2,1)}, bf16[4,64,1024]{2,1,0:T(8,128)(2,1)S(1)}, u32[]{:S(2)}, u32[]{:S(2)}) collective-permute-start(bf16[4,64,1024]{2,1,0:T(8,128)(2,1)} %get-tuple-element.10), channel_id=1, source_target_pairs={{0,3},{1,0},{2,1},{3,2},{4,7},{5,4},{6,5},{7,6},{8,11},{9,8},{10,9... | collective-permute-start | bytes 1572872 | tf_op jit(solution)/shard_map/ppermute | solution.py:245
  8.3 2.1 %send.1 = (f32[64,8,128]{2,1,0:T(8,128)}, f32[16,128]{1,0:T(8,128)}) custom-call(s32[1]{0:T(128)} %bitcast.tile, s32[64]{0:T(128)} %bitcast.14, s32[16]{0:T(128)} %counts.1, s32[16]{0:T(128)} %base_y.1, s32[16]{0:T(128)} %base_z.1, s32[16,128]{1,0:T(8,128)} %types.1, f32[3,16,128]{2,1,0:T(8,128)} %bitcast.13), custom_call_target="tpu_custom_call" | custom-call | tf_op jit(solution)/shard_map/send/pallas_call | solution.py:249
  10.4 0.0 copy-start.1
  10.4 13.8 %all-to-all-start = ((f32[64,8,128]{2,1,0:T(8,128)}), f32[64,8,128]{2,1,0:T(8,128)S(1)}, u32[]{:S(2)}, u32[]{:S(2)}) async-start(f32[64,8,128]{2,1,0:T(8,128)} %get-tuple-element.7), calls=%async_computation | async-start | bytes 524288 | tf_op jit(solution)/shard_map/all_to_all | solution.py:260
  24.2 0.0 collective-permute-done.left_a
  24.2 0.1 collective-permute-start.4
  24.3 0.0 collective-permute-done.3.right_b
  24.3 2.7 %collective-permute-start.5 = (bf16[4,64,1024]{2,1,0:T(8,128)(2,1)S(1)}, bf16[4,64,1024]{2,1,0:T(8,128)(2,1)}, u32[]{:S(2)}, u32[]{:S(2)}) collective-permute-start(bf16[4,64,1024]{2,1,0:T(8,128)(2,1)S(1)} %collective-permute-done.3.right_b), channel_id=1, source_target_pairs={{0,3},{1,0},{2,1},{3,2},{4,7},{5,4},{6,5},{7,6},{8,11},{9,8},{10,9... | collective-permute-start | bytes 1572872 | tf_op jit(solution)/shard_map/ppermute | solution.py:247
  27.0 9.2 %all-to-all-done.incoming = f32[64,8,128]{2,1,0:T(8,128)S(1)} async-done(((f32[64,8,128]{2,1,0:T(8,128)}), f32[64,8,128]{2,1,0:T(8,128)S(1)}, u32[]{:S(2)}, u32[]{:S(2)}) %all-to-all-start) | async-done | bytes 262176 | tf_op jit(solution)/shard_map/all_to_all | solution.py:260
  36.2 0.0 collective-permute-done.1.left_b
  36.2 0.0 collective-permute-done.2.right_a
  36.2 0.0 copy-done
  36.2 0.0 copy-done.1
  36.2 3.5 %near.1 = f32[64,128]{1,0:T(8,128)S(1)} custom-call(s32[1]{0:T(128)} %bitcast.tile, f32[64,8,128]{2,1,0:T(8,128)S(1)} %all-to-all-done.incoming, f32[8,16]{1,0:T(8,128)S(1)} %bitcast.10, bf16[8,64,1024]{2,1,0:T(8,128)(2,1)S(1)} %copy-done, bf16[4,64,1024]{2,1,0:T(8,128)(2,1)S(1)} %collective-permute-done.left_a, ...), custom_call_target="tpu_custom_call" | custom-call | flops 4000000000 | bytes 6291456 | tf_op jit(solution)/shard_map/near/pallas_call | solution.py:273
  39.7 0.0 collective-permute-done.4.far_a
  39.8 0.0 collective-permute-done.5.far_b
  39.8 3.1 %far.1 = f32[64,128]{1,0:T(8,128)S(1)} custom-call(s32[1]{0:T(128)} %bitcast.tile, f32[64,8,128]{2,1,0:T(8,128)S(1)} %all-to-all-done.incoming, f32[8,16]{1,0:T(8,128)S(1)} %bitcast.11, f32[64,128]{1,0:T(8,128)S(1)} %near.1, bf16[4,64,1024]{2,1,0:T(8,128)(2,1)} %collective-permute-done.4.far_a, bf16[4,64,1024]{2,1,0:T(8,128)(2,1)} %collective-permute-done.5.far_b), custom_call_target="tpu_custom_call" | custom-call | flops 1000000000 | bytes 2097152 | tf_op jit(solution)/shard_map/far/pallas_call | solution.py:289
  42.9 24.1 %all_to_all.17 = f32[64,1,128]{2,1,0:T(1,128)S(1)} all-to-all(f32[64,1,128]{2,1,0:T(1,128)S(1)} %bitcast.9), channel_id=1, replica_groups=mesh['slab'=64,'tile'=4] {'slab'}, dimensions={0} | all-to-all | bytes 65536 | tf_op jit(solution)/shard_map/all_to_all | solution.py:301
  67.0 0.0 copy-start.2
  67.0 0.1 mul.10
  67.1 0.6 copy-done.2
  67.7 0.6 multiply_reduce_fusion
Async XLA Ops:
  0.0 36.2 %copy-start = (bf16[8,64,1024]{2,1,0:T(8,128)(2,1)S(1)}, bf16[8,64,1024]{2,1,0:T(8,128)(2,1)}, u32[]{:S(2)}) copy-start(bf16[8,64,1024]{2,1,0:T(8,128)(2,1)} %own.1) | copy-start | bytes 3145732
  2.3 21.9 %collective-permute-start = (bf16[4,64,1024]{2,1,0:T(8,128)(2,1)}, bf16[4,64,1024]{2,1,0:T(8,128)(2,1)S(1)}, u32[]{:S(2)}, u32[]{:S(2)}) collective-permute-start(bf16[4,64,1024]{2,1,0:T(8,128)(2,1)} %get-tuple-element.10), channel_id=1, source_target_pairs={{0,1},{1,2},{2,3},{3,0},{4,5},{5,6},{6,7},{7,4},{8,9},{9,10},{10,1... | collective-permute-start | bytes 1572872 | tf_op jit(solution)/shard_map/ppermute | solution.py:242
  4.4 19.9 %collective-permute-start.3 = (bf16[4,64,1024]{2,1,0:T(8,128)(2,1)}, bf16[4,64,1024]{2,1,0:T(8,128)(2,1)S(1)}, u32[]{:S(2)}, u32[]{:S(2)}) collective-permute-start(bf16[4,64,1024]{2,1,0:T(8,128)(2,1)} %get-tuple-element.9), channel_id=1, source_target_pairs={{0,3},{1,0},{2,1},{3,2},{4,7},{5,4},{6,5},{7,6},{8,11},{9,8},{10,9... | collective-permute-start | bytes 1572872 | tf_op jit(solution)/shard_map/ppermute | solution.py:243
  5.6 30.5 %collective-permute-start.1 = (bf16[4,64,1024]{2,1,0:T(8,128)(2,1)}, bf16[4,64,1024]{2,1,0:T(8,128)(2,1)S(1)}, u32[]{:S(2)}, u32[]{:S(2)}) collective-permute-start(bf16[4,64,1024]{2,1,0:T(8,128)(2,1)} %get-tuple-element.9), channel_id=1, source_target_pairs={{0,1},{1,2},{2,3},{3,0},{4,5},{5,6},{6,7},{7,4},{8,9},{9,10},{10,1... | collective-permute-start | bytes 1572872 | tf_op jit(solution)/shard_map/ppermute | solution.py:244
  5.8 30.3 %collective-permute-start.2 = (bf16[4,64,1024]{2,1,0:T(8,128)(2,1)}, bf16[4,64,1024]{2,1,0:T(8,128)(2,1)S(1)}, u32[]{:S(2)}, u32[]{:S(2)}) collective-permute-start(bf16[4,64,1024]{2,1,0:T(8,128)(2,1)} %get-tuple-element.10), channel_id=1, source_target_pairs={{0,3},{1,0},{2,1},{3,2},{4,7},{5,4},{6,5},{7,6},{8,11},{9,8},{10,9... | collective-permute-start | bytes 1572872 | tf_op jit(solution)/shard_map/ppermute | solution.py:245
  10.4 25.8 %copy-start.1 = (f32[16,8]{0,1:T(8,128)S(1)}, f32[16,8]{0,1:T(8,128)}, u32[]{:S(2)}) copy-start(f32[16,8]{0,1:T(8,128)} %param.9) | copy-start | bytes 1540
  10.4 25.7 %all-to-all-start = ((f32[64,8,128]{2,1,0:T(8,128)}), f32[64,8,128]{2,1,0:T(8,128)S(1)}, u32[]{:S(2)}, u32[]{:S(2)}) async-start(f32[64,8,128]{2,1,0:T(8,128)} %get-tuple-element.7), calls=%async_computation | async-start | bytes 524288 | tf_op jit(solution)/shard_map/all_to_all | solution.py:260
  24.2 15.5 %collective-permute-start.4 = (bf16[4,64,1024]{2,1,0:T(8,128)(2,1)S(1)}, bf16[4,64,1024]{2,1,0:T(8,128)(2,1)}, u32[]{:S(2)}, u32[]{:S(2)}) collective-permute-start(bf16[4,64,1024]{2,1,0:T(8,128)(2,1)S(1)} %collective-permute-done.left_a), channel_id=1, source_target_pairs={{0,1},{1,2},{2,3},{3,0},{4,5},{5,6},{6,7},{7,4},{8,9},{9,10},{10,1... | collective-permute-start | bytes 1572872 | tf_op jit(solution)/shard_map/ppermute | solution.py:246
  24.3 15.4 %collective-permute-start.5 = (bf16[4,64,1024]{2,1,0:T(8,128)(2,1)S(1)}, bf16[4,64,1024]{2,1,0:T(8,128)(2,1)}, u32[]{:S(2)}, u32[]{:S(2)}) collective-permute-start(bf16[4,64,1024]{2,1,0:T(8,128)(2,1)S(1)} %collective-permute-done.3.right_b), channel_id=1, source_target_pairs={{0,3},{1,0},{2,1},{3,2},{4,7},{5,4},{6,5},{7,6},{8,11},{9,8},{10,9... | collective-permute-start | bytes 1572872 | tf_op jit(solution)/shard_map/ppermute | solution.py:247
  67.0 0.7 %copy-start.2 = (f32[16,128]{1,0:T(8,128)S(1)}, f32[16,128]{1,0:T(8,128)}, u32[]{:S(2)}) copy-start(f32[16,128]{1,0:T(8,128)} %get-tuple-element.8) | copy-start | bytes 24580
